TPU v7x, 32 devices: a whole 2x2x4 slice. The times are simulated.
32 devices in a mesh: section: 4 (over z), rep: 8 (over y, x, core).
Axes of the slice: x: 2, y: 2, z: 4, core: 2. Of those that a mesh axis runs over, the one named last changes fastest.
Arguments:
- tokens: bfloat16 [4, 1024, 1024], P(None, 'rep'), may hold values from -6 to 6
- replica_of_row: int32 [4, 1024, 1], P(None, 'rep'), may hold values from 0 to 15; in each aligned block of 128 rows (0 to 127, 128 to 255, ..., all dimensions but the last counted through in order) at most 12 rows name the same one
- widths: int32 [16], replicated, may hold values from 512 to 1024, as said below
- placement: int32 [16], replicated, may hold values from 0 to 23, as said below
- gains: float32 [4, 24, 1024], P('section', 'rep'), may hold values from 0.5 to 1.5
- weights: bfloat16 [4, 24, 1024, 1024], P('section', 'rep'), may hold values from -0.1875 to 0.1875
Outputs:
- final: bfloat16 [4, 1024, 1024], P(None, 'rep', 'section')
Inputs may be any that keep to these rules, and one draw needn't show every extreme that they name: `widths`: multiples of 128 from 512 to 1024. `placement`: distinct slots; slot g lies on index g // 3 of rep. `replica_of_row`: within the 128 tokens of one index of rep in one micro-batch, no replica is named by more than 12 tokens.
All inputs are finite; a program needn't handle non-finite values.
Results may differ from a plain program's by a relative error of at most 0.008.
Values may be sent and summed in bfloat16 or wider, within the bound.
No kernel may reach another device: no remote copies, remote signals or barrier semaphores. Data moves between devices by JAX's collectives and lax.ppermute only.
A program may use at most 64 MiB of HBM per device.

v0:
```python
import jax
import jax.numpy as jnp
from jax import lax
from jax.sharding import PartitionSpec as P

epsilon = 1e-05


def shifted(x, axis, by):
    length = lax.axis_size(axis)
    pairs = [(i, i + by) for i in range(length) if 0 <= i + by < length]
    return lax.ppermute(x, axis, pairs)


def on_device(tokens, replica_of_row, widths, placement, gains, weights):
    batches, row_count, width_max = tokens.shape
    rep_count = lax.axis_size("rep")
    section_count = lax.axis_size("section")
    slot_count = weights.shape[1]
    replica_count = widths.shape[0]
    total_slots = slot_count * rep_count
    capacity = (3 * row_count + 2 * replica_count - 1) // (2 * replica_count)
    section_id = lax.axis_index("section")
    rep_id = lax.axis_index("rep")
    final_section = section_count - 1
    features = jnp.arange(width_max, dtype=jnp.int32)
    replica_ids = jnp.arange(replica_count, dtype=jnp.int32)
    global_ids = rep_id * slot_count + jnp.arange(slot_count, dtype=jnp.int32)
    slot_width = jnp.sum(
        (placement[None, :] == global_ids[:, None]).astype(jnp.int32) * widths[None, :], axis=1
    )
    slot_live = (features[None, :] < slot_width[:, None]).astype(jnp.float32)
    slot_scale = 1.0 / jnp.maximum(slot_width, 1).astype(jnp.float32)
    section_gain = gains[0]
    section_weight = weights[0]
    slot_targets = jnp.arange(total_slots * capacity, dtype=jnp.int32)
    slot_numbers = jnp.arange(total_slots, dtype=jnp.int32)

    def routing(row_replica):
        picked = (row_replica[:, None] == replica_ids[None, :]).astype(jnp.int32)
        slot_of_row = jnp.sum(picked * placement[None, :], axis=1)
        row_width = jnp.sum(picked * widths[None, :], axis=1)
        slot_hits = (slot_of_row[:, None] == slot_numbers[None, :]).astype(jnp.int32)
        earlier = jnp.cumsum(slot_hits, axis=0) - slot_hits
        position = jnp.sum(earlier * slot_hits, axis=1)
        target = slot_of_row * capacity + position
        routing_table = (slot_targets[:, None] == target[None, :]).astype(jnp.bfloat16)
        return (routing_table, row_width)

    def update(buffer):
        float_rows = buffer.astype(jnp.float32)
        mean_square = jnp.sum(float_rows * float_rows, axis=-1) * slot_scale[None, :, None]
        lowered = (
            float_rows
            * lax.rsqrt(mean_square + epsilon)[..., None]
            * section_gain[None, :, None, :]
        ).astype(jnp.bfloat16)
        projected = jnp.einsum(
            "nscd,sde->nsce", lowered, section_weight, preferred_element_type=jnp.float32
        )
        return (float_rows + jax.nn.silu(projected) * slot_live[None, :, None, :]).astype(
            jnp.bfloat16
        )

    def unchanged(buffer):
        return buffer

    tick_count = batches + section_count - 1
    routing_tables, row_widths = jax.vmap(routing)(replica_of_row[:, :, 0])
    entering = jnp.where(
        features[None, None, :] < row_widths[:, :, None], tokens, jnp.zeros((), jnp.bfloat16)
    )
    outgoing = jnp.einsum(
        "mgr,mrd->mgd", routing_tables, entering, preferred_element_type=jnp.float32
    ).astype(jnp.bfloat16)
    outgoing = outgoing.reshape(batches, rep_count, slot_count * capacity, width_max)
    arrived_all = lax.all_to_all(outgoing, "rep", split_axis=1, concat_axis=1, tiled=True)
    arrived_all = arrived_all.reshape(batches, rep_count, slot_count, capacity, width_max)

    def tick(counter, carry):
        incoming, outbuf = carry
        index = counter - section_id
        valid = (index >= 0) & (index < batches)
        clipped = jnp.clip(index, 0, batches - 1)
        first_input = lax.dynamic_index_in_dim(arrived_all, clipped, 0, keepdims=False)
        current = jnp.where(section_id == 0, first_input, incoming)
        updated = lax.cond(valid, update, unchanged, current)
        storing = valid & (section_id == final_section)
        stored = lax.dynamic_update_index_in_dim(outbuf, updated, clipped, 0)
        outbuf = jnp.where(storing, stored, outbuf)
        incoming = shifted(updated, "section", 1)
        return (incoming, outbuf)

    start_slots = jnp.zeros((rep_count, slot_count, capacity, width_max), jnp.bfloat16)
    start_out = jnp.zeros((batches, rep_count, slot_count, capacity, width_max), jnp.bfloat16)
    last_slots, slot_results = lax.fori_loop(0, tick_count, tick, (start_slots, start_out))
    returned = lax.all_to_all(
        slot_results.reshape(batches, rep_count, slot_count * capacity, width_max),
        "rep",
        split_axis=1,
        concat_axis=1,
        tiled=True,
    )
    flat_back = returned.reshape(batches, total_slots * capacity, width_max)
    final_rows = jnp.einsum(
        "mgr,mgd->mrd", routing_tables, flat_back, preferred_element_type=jnp.float32
    ).astype(jnp.bfloat16)
    contribution = jnp.where(
        section_id == final_section, final_rows.astype(jnp.float32), jnp.zeros((), jnp.float32)
    )
    gathered = lax.psum_scatter(
        contribution.astype(jnp.bfloat16), "section", scatter_dimension=2, tiled=True
    )
    return gathered


def solution(mesh):
    placed = (
        P(None, "rep", None),
        P(None, "rep", None),
        P(),
        P(),
        P("section", "rep", None),
        P("section", "rep", None, None),
    )
    return jax.shard_map(
        on_device, mesh=mesh, in_specs=placed, out_specs=P(None, "rep", "section"), check_vma=False
    )
```

profile of v0, /device:TPU:0, one launch (start us, length us, event | category | flops | bytes accessed | tf_op | source)
XLA Modules:
  0.0 275.3 jit_solution(11272264600902718)
XLA Ops:
  6.5 0.8 select_reduce_fusion.2
  8.0 2.1 convolution_convert_fusion
  10.1 3.2 %copy.37 = bf16[4,288,1024]{2,0,1:T(4,128)(2,1)} copy(bf16[4,288,1024]{2,1,0:T(8,128)(2,1)S(1)} %convolution_convert_fusion) | data formatting | bytes 4718592 | tf_op jit(solution)/shard_map/convert_element_type | solution.py:75
  13.3 5.3 %all-to-all-start = ((bf16[4,8,36,1024]{3,0,2,1:T(4,128)(2,1)}), bf16[4,8,36,1024]{3,0,2,1:T(4,128)(2,1)S(1)}, u32[]{:S(2)}, u32[]{:S(2)}) async-start(bf16[4,8,36,1024]{3,0,2,1:T(4,128)(2,1)} %bitcast.37), calls=%async_computation | async-start | bytes 4718592 | tf_op jit(solution)/shard_map/all_to_all | solution.py:77
  19.0 29.1 %all-to-all-done = bf16[4,8,36,1024]{3,0,2,1:T(4,128)(2,1)S(1)} async-done(((bf16[4,8,36,1024]{3,0,2,1:T(4,128)(2,1)}), bf16[4,8,36,1024]{3,0,2,1:T(4,128)(2,1)S(1)}, u32[]{:S(2)}, u32[]{:S(2)}) %all-to-all-start) | async-done | bytes 2359328 | tf_op jit(solution)/shard_map/all_to_all | solution.py:77
  48.1 2.7 copy.38
  50.9 1.7 broadcast_in_dim.47.clone
  52.6 129.7 %while.17 = (s32[]{:T(128)}, bf16[8,3,12,1024]{3,0,2,1:T(8,128)(2,1)S(1)}, bf16[4,8,3,12,1024]{4,1,3,2,0:T(8,128)(2,1)}, s32[]{:T(128)}, pred[]{:T(512)}, /*inde...) while((s32[]{:T(128)}, ...), condition=%wide.region_9.10_spmd.clone, body=%wide.region_5.9_spmd.clone.sunk | while | flops 608999680 | bytes 19899208 | solution.py:96
  52.6 1.3 constant_dynamic-slice_fusion.3
  54.0 0.6 bitcast_select_fusion.2
  54.6 4.7 %conditional.3 = (bf16[8,3,12,1024]{3,2,0,1:T(8,128)(2,1)S(1)}) conditional(s32[]{:T(128)} %convert_element_type.86, bf16[8,3,12,1024]{3,2,0,1:T(8,128)(2,1)S(1)} %bitcast_select_fusion.2, (bf16[8,3,12,1024]{3,2,0,1:T(8,128)(2,1)S(1)}, f32[3]{0:T(128)S(1)}, f32[1,3,1024]{2,1,0:T(4,128)S(1)}, bf16[3,1024,1024]{2,1,0:T(8,128)(2,1)}, ...), branch_computations={%region_6.6_spmd, %region_7.8_spmd} | conditional | flops 608403712 | bytes 9269780 | solution.py:87
  55.0 4.3 %fusion.7 = bf16[8,3,12,1024]{3,2,0,1:T(8,128)(2,1)S(1)} fusion(bf16[8,3,12,1024]{3,2,0,1:T(8,128)(2,1)S(1)} %copy.80, bf16[3,1024,1024]{2,1,0:T(8,128)(2,1)} %get-tuple-element.218, f32[3,1024]{1,0:T(4,128)S(1)} %get-tuple-element.219, f32[3,1024]{1,0:T(4,128)S(1)} %bitcast.39, f32[8,3,12]{2,0,1:T(8,128)S(1)} %add_rsqrt_fusion), kind=kOutput, calls=%fused_computation.9 | convolution fusion | flops 607518720 | bytes 7496832 | tf_op jit(solution)/shard_map/while/body/eval_jaxpr/cond/branch_1_fun/nscd,sde->nsce/dot_general | solution.py:58
  59.4 0.3 copy.66
  59.7 1.3 collective-permute-start
  61.0 0.4 copy_select_fusion.2
  61.4 1.2 copy_dynamic-update-slice_fusion.2
  62.6 8.5 %collective-permute-done = bf16[8,3,12,1024]{3,0,2,1:T(8,128)(2,1)S(1)} collective-permute-done((bf16[8,3,12,1024]{3,0,2,1:T(8,128)(2,1)S(1)}, bf16[8,3,12,1024]{3,0,2,1:T(8,128)(2,1)S(1)}, u32[]{:S(2)}, u32[]{:S(2)}) %collective-permute-start) | collective-permute-done | bytes 589856 | tf_op jit(solution)/shard_map/while/body/eval_jaxpr/ppermute | solution.py:12
  71.2 1.3 constant_dynamic-slice_fusion.3
  72.5 0.6 bitcast_select_fusion.2
  73.1 4.7 %conditional.3 = (bf16[8,3,12,1024]{3,2,0,1:T(8,128)(2,1)S(1)}) conditional(s32[]{:T(128)} %convert_element_type.86, bf16[8,3,12,1024]{3,2,0,1:T(8,128)(2,1)S(1)} %bitcast_select_fusion.2, (bf16[8,3,12,1024]{3,2,0,1:T(8,128)(2,1)S(1)}, f32[3]{0:T(128)S(1)}, f32[1,3,1024]{2,1,0:T(4,128)S(1)}, bf16[3,1024,1024]{2,1,0:T(8,128)(2,1)}, ...), branch_computations={%region_6.6_spmd, %region_7.8_spmd} | conditional | flops 608403712 | bytes 9269780 | solution.py:87
  73.5 4.3 %fusion.7 = bf16[8,3,12,1024]{3,2,0,1:T(8,128)(2,1)S(1)} fusion(bf16[8,3,12,1024]{3,2,0,1:T(8,128)(2,1)S(1)} %copy.80, bf16[3,1024,1024]{2,1,0:T(8,128)(2,1)} %get-tuple-element.218, f32[3,1024]{1,0:T(4,128)S(1)} %get-tuple-element.219, f32[3,1024]{1,0:T(4,128)S(1)} %bitcast.39, f32[8,3,12]{2,0,1:T(8,128)S(1)} %add_rsqrt_fusion), kind=kOutput, calls=%fused_computation.9 | convolution fusion | flops 607518720 | bytes 7496832 | tf_op jit(solution)/shard_map/while/body/eval_jaxpr/cond/branch_1_fun/nscd,sde->nsce/dot_general | solution.py:58
  77.9 0.3 copy.66
  78.2 4.4 %collective-permute-start = (bf16[8,3,12,1024]{3,0,2,1:T(8,128)(2,1)S(1)}, bf16[8,3,12,1024]{3,0,2,1:T(8,128)(2,1)S(1)}, u32[]{:S(2)}, u32[]{:S(2)}) collective-permute-start(bf16[8,3,12,1024]{3,0,2,1:T(8,128)(2,1)S(1)} %copy.66), channel_id=1, source_target_pairs={{0,8},{8,16},{16,24},{1,9},{9,17},{17,25},{2,10},{10,18},{18,26},{... | collective-permute-start | bytes 1769480 | tf_op jit(solution)/shard_map/while/body/eval_jaxpr/ppermute | solution.py:12
  82.6 0.4 copy_select_fusion.2
  83.0 1.2 copy_dynamic-update-slice_fusion.2
  84.2 7.7 %collective-permute-done = bf16[8,3,12,1024]{3,0,2,1:T(8,128)(2,1)S(1)} collective-permute-done((bf16[8,3,12,1024]{3,0,2,1:T(8,128)(2,1)S(1)}, bf16[8,3,12,1024]{3,0,2,1:T(8,128)(2,1)S(1)}, u32[]{:S(2)}, u32[]{:S(2)}) %collective-permute-start) | collective-permute-done | bytes 589856 | tf_op jit(solution)/shard_map/while/body/eval_jaxpr/ppermute | solution.py:12
  91.9 1.3 constant_dynamic-slice_fusion.3
  93.2 0.6 bitcast_select_fusion.2
  93.9 4.7 %conditional.3 = (bf16[8,3,12,1024]{3,2,0,1:T(8,128)(2,1)S(1)}) conditional(s32[]{:T(128)} %convert_element_type.86, bf16[8,3,12,1024]{3,2,0,1:T(8,128)(2,1)S(1)} %bitcast_select_fusion.2, (bf16[8,3,12,1024]{3,2,0,1:T(8,128)(2,1)S(1)}, f32[3]{0:T(128)S(1)}, f32[1,3,1024]{2,1,0:T(4,128)S(1)}, bf16[3,1024,1024]{2,1,0:T(8,128)(2,1)}, ...), branch_computations={%region_6.6_spmd, %region_7.8_spmd} | conditional | flops 608403712 | bytes 9269780 | solution.py:87
  94.3 4.3 %fusion.7 = bf16[8,3,12,1024]{3,2,0,1:T(8,128)(2,1)S(1)} fusion(bf16[8,3,12,1024]{3,2,0,1:T(8,128)(2,1)S(1)} %copy.80, bf16[3,1024,1024]{2,1,0:T(8,128)(2,1)} %get-tuple-element.218, f32[3,1024]{1,0:T(4,128)S(1)} %get-tuple-element.219, f32[3,1024]{1,0:T(4,128)S(1)} %bitcast.39, f32[8,3,12]{2,0,1:T(8,128)S(1)} %add_rsqrt_fusion), kind=kOutput, calls=%fused_computation.9 | convolution fusion | flops 607518720 | bytes 7496832 | tf_op jit(solution)/shard_map/while/body/eval_jaxpr/cond/branch_1_fun/nscd,sde->nsce/dot_general | solution.py:58
  99.0 4.4 %collective-permute-start = (bf16[8,3,12,1024]{3,0,2,1:T(8,128)(2,1)S(1)}, bf16[8,3,12,1024]{3,0,2,1:T(8,128)(2,1)S(1)}, u32[]{:S(2)}, u32[]{:S(2)}) collective-permute-start(bf16[8,3,12,1024]{3,0,2,1:T(8,128)(2,1)S(1)} %copy.66), channel_id=1, source_target_pairs={{0,8},{8,16},{16,24},{1,9},{9,17},{17,25},{2,10},{10,18},{18,26},{... | collective-permute-start | bytes 1769480 | tf_op jit(solution)/shard_map/while/body/eval_jaxpr/ppermute | solution.py:12
  103.4 0.4 copy_select_fusion.2
  103.8 1.2 copy_dynamic-update-slice_fusion.2
  104.9 6.8 %collective-permute-done = bf16[8,3,12,1024]{3,0,2,1:T(8,128)(2,1)S(1)} collective-permute-done((bf16[8,3,12,1024]{3,0,2,1:T(8,128)(2,1)S(1)}, bf16[8,3,12,1024]{3,0,2,1:T(8,128)(2,1)S(1)}, u32[]{:S(2)}, u32[]{:S(2)}) %collective-permute-start) | collective-permute-done | bytes 589856 | tf_op jit(solution)/shard_map/while/body/eval_jaxpr/ppermute | solution.py:12
  111.8 1.3 constant_dynamic-slice_fusion.3
  113.1 0.6 bitcast_select_fusion.2
  113.8 4.7 %conditional.3 = (bf16[8,3,12,1024]{3,2,0,1:T(8,128)(2,1)S(1)}) conditional(s32[]{:T(128)} %convert_element_type.86, bf16[8,3,12,1024]{3,2,0,1:T(8,128)(2,1)S(1)} %bitcast_select_fusion.2, (bf16[8,3,12,1024]{3,2,0,1:T(8,128)(2,1)S(1)}, f32[3]{0:T(128)S(1)}, f32[1,3,1024]{2,1,0:T(4,128)S(1)}, bf16[3,1024,1024]{2,1,0:T(8,128)(2,1)}, ...), branch_computations={%region_6.6_spmd, %region_7.8_spmd} | conditional | flops 608403712 | bytes 9269780 | solution.py:87
  114.2 4.3 %fusion.7 = bf16[8,3,12,1024]{3,2,0,1:T(8,128)(2,1)S(1)} fusion(bf16[8,3,12,1024]{3,2,0,1:T(8,128)(2,1)S(1)} %copy.80, bf16[3,1024,1024]{2,1,0:T(8,128)(2,1)} %get-tuple-element.218, f32[3,1024]{1,0:T(4,128)S(1)} %get-tuple-element.219, f32[3,1024]{1,0:T(4,128)S(1)} %bitcast.39, f32[8,3,12]{2,0,1:T(8,128)S(1)} %add_rsqrt_fusion), kind=kOutput, calls=%fused_computation.9 | convolution fusion | flops 607518720 | bytes 7496832 | tf_op jit(solution)/shard_map/while/body/eval_jaxpr/cond/branch_1_fun/nscd,sde->nsce/dot_general | solution.py:58
  118.9 4.4 %collective-permute-start = (bf16[8,3,12,1024]{3,0,2,1:T(8,128)(2,1)S(1)}, bf16[8,3,12,1024]{3,0,2,1:T(8,128)(2,1)S(1)}, u32[]{:S(2)}, u32[]{:S(2)}) collective-permute-start(bf16[8,3,12,1024]{3,0,2,1:T(8,128)(2,1)S(1)} %copy.66), channel_id=1, source_target_pairs={{0,8},{8,16},{16,24},{1,9},{9,17},{17,25},{2,10},{10,18},{18,26},{... | collective-permute-start | bytes 1769480 | tf_op jit(solution)/shard_map/while/body/eval_jaxpr/ppermute | solution.py:12
  123.3 0.4 copy_select_fusion.2
  123.7 1.2 copy_dynamic-update-slice_fusion.2
  124.8 6.0 %collective-permute-done = bf16[8,3,12,1024]{3,0,2,1:T(8,128)(2,1)S(1)} collective-permute-done((bf16[8,3,12,1024]{3,0,2,1:T(8,128)(2,1)S(1)}, bf16[8,3,12,1024]{3,0,2,1:T(8,128)(2,1)S(1)}, u32[]{:S(2)}, u32[]{:S(2)}) %collective-permute-start) | collective-permute-done | bytes 589856 | tf_op jit(solution)/shard_map/while/body/eval_jaxpr/ppermute | solution.py:12
  130.9 1.3 constant_dynamic-slice_fusion.3
  132.2 0.6 bitcast_select_fusion.2
  133.2 9.1 %collective-permute-start = (bf16[8,3,12,1024]{3,0,2,1:T(8,128)(2,1)S(1)}, bf16[8,3,12,1024]{3,0,2,1:T(8,128)(2,1)S(1)}, u32[]{:S(2)}, u32[]{:S(2)}) collective-permute-start(bf16[8,3,12,1024]{3,0,2,1:T(8,128)(2,1)S(1)} %copy.66), channel_id=1, source_target_pairs={{0,8},{8,16},{16,24},{1,9},{9,17},{17,25},{2,10},{10,18},{18,26},{... | collective-permute-start | bytes 1769480 | tf_op jit(solution)/shard_map/while/body/eval_jaxpr/ppermute | solution.py:12
  142.3 0.4 copy_select_fusion.2
  142.7 1.2 copy_dynamic-update-slice_fusion.2
  143.9 6.1 %collective-permute-done = bf16[8,3,12,1024]{3,0,2,1:T(8,128)(2,1)S(1)} collective-permute-done((bf16[8,3,12,1024]{3,0,2,1:T(8,128)(2,1)S(1)}, bf16[8,3,12,1024]{3,0,2,1:T(8,128)(2,1)S(1)}, u32[]{:S(2)}, u32[]{:S(2)}) %collective-permute-start) | collective-permute-done | bytes 589856 | tf_op jit(solution)/shard_map/while/body/eval_jaxpr/ppermute | solution.py:12
  150.1 1.3 constant_dynamic-slice_fusion.3
  151.4 0.6 bitcast_select_fusion.2
  152.4 4.4 %collective-permute-start = (bf16[8,3,12,1024]{3,0,2,1:T(8,128)(2,1)S(1)}, bf16[8,3,12,1024]{3,0,2,1:T(8,128)(2,1)S(1)}, u32[]{:S(2)}, u32[]{:S(2)}) collective-permute-start(bf16[8,3,12,1024]{3,0,2,1:T(8,128)(2,1)S(1)} %copy.66), channel_id=1, source_target_pairs={{0,8},{8,16},{16,24},{1,9},{9,17},{17,25},{2,10},{10,18},{18,26},{... | collective-permute-start | bytes 1769480 | tf_op jit(solution)/shard_map/while/body/eval_jaxpr/ppermute | solution.py:12
  156.8 0.4 copy_select_fusion.2
  157.2 1.2 copy_dynamic-update-slice_fusion.2
  158.4 5.8 %collective-permute-done = bf16[8,3,12,1024]{3,0,2,1:T(8,128)(2,1)S(1)} collective-permute-done((bf16[8,3,12,1024]{3,0,2,1:T(8,128)(2,1)S(1)}, bf16[8,3,12,1024]{3,0,2,1:T(8,128)(2,1)S(1)}, u32[]{:S(2)}, u32[]{:S(2)}) %collective-permute-start) | collective-permute-done | bytes 589856 | tf_op jit(solution)/shard_map/while/body/eval_jaxpr/ppermute | solution.py:12
  164.2 1.3 constant_dynamic-slice_fusion.3
  165.6 0.6 bitcast_select_fusion.2
  166.6 8.4 %collective-permute-start = (bf16[8,3,12,1024]{3,0,2,1:T(8,128)(2,1)S(1)}, bf16[8,3,12,1024]{3,0,2,1:T(8,128)(2,1)S(1)}, u32[]{:S(2)}, u32[]{:S(2)}) collective-permute-start(bf16[8,3,12,1024]{3,0,2,1:T(8,128)(2,1)S(1)} %copy.66), channel_id=1, source_target_pairs={{0,8},{8,16},{16,24},{1,9},{9,17},{17,25},{2,10},{10,18},{18,26},{... | collective-permute-start | bytes 1769480 | tf_op jit(solution)/shard_map/while/body/eval_jaxpr/ppermute | solution.py:12
  175.0 0.4 copy_select_fusion.2
  175.3 1.2 copy_dynamic-update-slice_fusion.2
  176.5 5.8 %collective-permute-done = bf16[8,3,12,1024]{3,0,2,1:T(8,128)(2,1)S(1)} collective-permute-done((bf16[8,3,12,1024]{3,0,2,1:T(8,128)(2,1)S(1)}, bf16[8,3,12,1024]{3,0,2,1:T(8,128)(2,1)S(1)}, u32[]{:S(2)}, u32[]{:S(2)}) %collective-permute-start) | collective-permute-done | bytes 589856 | tf_op jit(solution)/shard_map/while/body/eval_jaxpr/ppermute | solution.py:12
  182.3 3.5 %copy.41 = bf16[4,8,36,1024]{3,0,2,1:T(4,128)(2,1)S(1)} copy(bf16[4,8,36,1024]{3,1,2,0:T(8,128)(2,1)} %bitcast.8) | data formatting | bytes 4718592 | tf_op jit(solution)/shard_map/reshape | solution.py:98
  185.8 46.8 %all_to_all.10 = bf16[4,8,36,1024]{3,0,2,1:T(4,128)(2,1)S(1)} all-to-all(bf16[4,8,36,1024]{3,0,2,1:T(4,128)(2,1)S(1)} %copy.41), channel_id=1, replica_groups=mesh['section'=4,'rep'=8] {'rep'}, dimensions={1} | all-to-all | bytes 4718592 | tf_op jit(solution)/shard_map/all_to_all | solution.py:97
  232.6 2.6 select_convert_fusion
  235.3 33.2 %reduce-scatter.2.cloned.1.call-done = bf16[4,128,256]{2,1,0:T(8,128)(2,1)} async-done(((bf16[4,128,1024]{2,1,0:T(8,128)(2,1)}), bf16[4,128,256]{2,1,0:T(8,128)(2,1)}) %reduce-scatter.2.cloned.1.call-update) | async-done | bytes 262160 | tf_op jit(solution)/shard_map/reduce_scatter | solution.py:111
  (44 shorter events, 4.7 us)
Async XLA Ops:
  13.3 5.4 %copy-start = (f32[1,3,1024]{2,0,1:T(1,128)S(1)}, f32[1,3,1024]{2,0,1:T(1,128)}, u32[]{:S(2)}) copy-start(f32[1,3,1024]{2,0,1:T(1,128)} %param.14) | copy-start | bytes 36868
  13.3 5.4 %copy-start.1 = (s32[16]{0:T(128)S(1)}, s32[16]{0:T(128)}, u32[]{:S(2)}) copy-start(s32[16]{0:T(128)} %param.13) | copy-start | bytes 196
  13.3 5.4 %copy-start.2 = (s32[16]{0:T(128)S(1)}, s32[16]{0:T(128)}, u32[]{:S(2)}) copy-start(s32[16]{0:T(128)} %param.12) | copy-start | bytes 196
  13.3 34.8 %all-to-all-start = ((bf16[4,8,36,1024]{3,0,2,1:T(4,128)(2,1)}), bf16[4,8,36,1024]{3,0,2,1:T(4,128)(2,1)S(1)}, u32[]{:S(2)}, u32[]{:S(2)}) async-start(bf16[4,8,36,1024]{3,0,2,1:T(4,128)(2,1)} %bitcast.37), calls=%async_computation | async-start | bytes 4718592 | tf_op jit(solution)/shard_map/all_to_all | solution.py:77
  18.7 249.7 %reduce-scatter.2.cloned.1.call-start = ((), (), s32[]{:S(2)}) async-start(), calls=%async_computation.3 | async-start | bytes 1310720 | tf_op jit(solution)/shard_map/reduce_scatter | solution.py:111
  59.7 11.4 %collective-permute-start = (bf16[8,3,12,1024]{3,0,2,1:T(8,128)(2,1)S(1)}, bf16[8,3,12,1024]{3,0,2,1:T(8,128)(2,1)S(1)}, u32[]{:S(2)}, u32[]{:S(2)}) collective-permute-start(bf16[8,3,12,1024]{3,0,2,1:T(8,128)(2,1)S(1)} %copy.66), channel_id=1, source_target_pairs={{0,8},{8,16},{16,24},{1,9},{9,17},{17,25},{2,10},{10,18},{18,26},{... | collective-permute-start | bytes 1769480 | tf_op jit(solution)/shard_map/while/body/eval_jaxpr/ppermute | solution.py:12
  78.2 13.6 %collective-permute-start = (bf16[8,3,12,1024]{3,0,2,1:T(8,128)(2,1)S(1)}, bf16[8,3,12,1024]{3,0,2,1:T(8,128)(2,1)S(1)}, u32[]{:S(2)}, u32[]{:S(2)}) collective-permute-start(bf16[8,3,12,1024]{3,0,2,1:T(8,128)(2,1)S(1)} %copy.66), channel_id=1, source_target_pairs={{0,8},{8,16},{16,24},{1,9},{9,17},{17,25},{2,10},{10,18},{18,26},{... | collective-permute-start | bytes 1769480 | tf_op jit(solution)/shard_map/while/body/eval_jaxpr/ppermute | solution.py:12
  99.0 12.8 %collective-permute-start = (bf16[8,3,12,1024]{3,0,2,1:T(8,128)(2,1)S(1)}, bf16[8,3,12,1024]{3,0,2,1:T(8,128)(2,1)S(1)}, u32[]{:S(2)}, u32[]{:S(2)}) collective-permute-start(bf16[8,3,12,1024]{3,0,2,1:T(8,128)(2,1)S(1)} %copy.66), channel_id=1, source_target_pairs={{0,8},{8,16},{16,24},{1,9},{9,17},{17,25},{2,10},{10,18},{18,26},{... | collective-permute-start | bytes 1769480 | tf_op jit(solution)/shard_map/while/body/eval_jaxpr/ppermute | solution.py:12
  118.9 11.9 %collective-permute-start = (bf16[8,3,12,1024]{3,0,2,1:T(8,128)(2,1)S(1)}, bf16[8,3,12,1024]{3,0,2,1:T(8,128)(2,1)S(1)}, u32[]{:S(2)}, u32[]{:S(2)}) collective-permute-start(bf16[8,3,12,1024]{3,0,2,1:T(8,128)(2,1)S(1)} %copy.66), channel_id=1, source_target_pairs={{0,8},{8,16},{16,24},{1,9},{9,17},{17,25},{2,10},{10,18},{18,26},{... | collective-permute-start | bytes 1769480 | tf_op jit(solution)/shard_map/while/body/eval_jaxpr/ppermute | solution.py:12
  133.2 16.8 %collective-permute-start = (bf16[8,3,12,1024]{3,0,2,1:T(8,128)(2,1)S(1)}, bf16[8,3,12,1024]{3,0,2,1:T(8,128)(2,1)S(1)}, u32[]{:S(2)}, u32[]{:S(2)}) collective-permute-start(bf16[8,3,12,1024]{3,0,2,1:T(8,128)(2,1)S(1)} %copy.66), channel_id=1, source_target_pairs={{0,8},{8,16},{16,24},{1,9},{9,17},{17,25},{2,10},{10,18},{18,26},{... | collective-permute-start | bytes 1769480 | tf_op jit(solution)/shard_map/while/body/eval_jaxpr/ppermute | solution.py:12
  152.4 11.8 %collective-permute-start = (bf16[8,3,12,1024]{3,0,2,1:T(8,128)(2,1)S(1)}, bf16[8,3,12,1024]{3,0,2,1:T(8,128)(2,1)S(1)}, u32[]{:S(2)}, u32[]{:S(2)}) collective-permute-start(bf16[8,3,12,1024]{3,0,2,1:T(8,128)(2,1)S(1)} %copy.66), channel_id=1, source_target_pairs={{0,8},{8,16},{16,24},{1,9},{9,17},{17,25},{2,10},{10,18},{18,26},{... | collective-permute-start | bytes 1769480 | tf_op jit(solution)/shard_map/while/body/eval_jaxpr/ppermute | solution.py:12
  166.6 15.7 %collective-permute-start = (bf16[8,3,12,1024]{3,0,2,1:T(8,128)(2,1)S(1)}, bf16[8,3,12,1024]{3,0,2,1:T(8,128)(2,1)S(1)}, u32[]{:S(2)}, u32[]{:S(2)}) collective-permute-start(bf16[8,3,12,1024]{3,0,2,1:T(8,128)(2,1)S(1)} %copy.66), channel_id=1, source_target_pairs={{0,8},{8,16},{16,24},{1,9},{9,17},{17,25},{2,10},{10,18},{18,26},{... | collective-permute-start | bytes 1769480 | tf_op jit(solution)/shard_map/while/body/eval_jaxpr/ppermute | solution.py:12
Sparse Core Ops, SparseCore 0:
  235.4 32.9 reduce-scatter.1
where the time goes:
time: 276 us; the launch traced here: 275 us
  waiting for transfers between devices  109 us (39%)
  blocking collectives  46.8 us (17%)
  starting transfers between devices  41.9 us (15%)
  local copies, waits for them, and re-layouts  31.1 us (11%)
  matrix products  22 us (8%)
  between operations  13.5 us (5%)
  other arithmetic  10.4 us (4%)
    all_to_all x1, blocking collectives, on_device(): lax.all_to_all(slot_results.reshape(batches, rep_count, slot_count * capa...  46.8 us
    ppermute x7, waiting for transfers between devices, shifted(): return lax.ppermute(x, axis, pairs)  46.8 us
    ppermute x7, starting transfers between devices, shifted(): return lax.ppermute(x, axis, pairs)  36.5 us
    reduce_scatter x1, waiting for transfers between devices, on_device(): lax.psum_scatter(contribution.astype(jnp.bfloat16), 'section', scatter_di...  33.2 us
    all_to_all x1, waiting for transfers between devices, on_device(): lax.all_to_all(outgoing, 'rep', split_axis=1, concat_axis=1, tiled=True)  29.1 us
    select_n x14, local copies, waits for them, and re-layouts, tick(): outbuf = jnp.where(storing, stored, outbuf)  17.3 us
    dot_general x4, matrix products, update(): jnp.einsum('nscd,sde->nsce', lowered, section_weight, preferred_element_t...  17.3 us
  transfers between devices with their start and end apart: 9, of which 9 were waited for; matrix products, arithmetic and copies ran while one was open for 4% of the time, Pallas kernels for 0%

commit v1 on v0

--- a/solution.py
+++ b/solution.py
@@ -94,13 +94,11 @@
     start_slots = jnp.zeros((rep_count, slot_count, capacity, width_max), jnp.bfloat16)
     start_out = jnp.zeros((batches, rep_count, slot_count, capacity, width_max), jnp.bfloat16)
     last_slots, slot_results = lax.fori_loop(0, tick_count, tick, (start_slots, start_out))
-    returned = lax.all_to_all(
-        slot_results.reshape(batches, rep_count, slot_count * capacity, width_max),
-        "rep",
-        split_axis=1,
-        concat_axis=1,
-        tiled=True,
-    )
+    value = slot_results.reshape(batches, rep_count, slot_count * capacity, width_max)
+    size = lax.axis_size("rep")
+    pieces = jnp.stack(jnp.split(value, size, axis=1), axis=0)
+    pieces = lax.all_to_all(pieces, "rep", split_axis=0, concat_axis=0)
+    returned = jnp.concatenate(pieces, axis=1)
     flat_back = returned.reshape(batches, total_slots * capacity, width_max)
     final_rows = jnp.einsum(
         "mgr,mgd->mrd", routing_tables, flat_back, preferred_element_type=jnp.float32

time: 276 us -> 290 us (1.051)
  local copies, waits for them, and re-layouts: 31.1 us -> 44.9 us
    split x0 -> x1, local copies, waits for them, and re-layouts: none -> 14.2 us  [on_device(): pieces = jnp.stack(jnp.split(value, size, axis=1), axis=0)]
    reshape x1 -> x0, local copies, waits for them, and re-layouts: 3.49 us -> none  [on_device(): slot_results.reshape(batches, rep_count, slot_count * capacity, width_max)]
where the time goes in v1:
time: 290 us; the launch traced here: 289 us
  waiting for transfers between devices  109 us (38%)
  blocking collectives  46.8 us (16%)
  local copies, waits for them, and re-layouts  44.9 us (15%)
  starting transfers between devices  42.1 us (15%)
  matrix products  22.1 us (8%)
  between operations  13.5 us (5%)
  other arithmetic  10.4 us (4%)
    ppermute x7, waiting for transfers between devices, shifted(): return lax.ppermute(x, axis, pairs)  46.9 us
    all_to_all x1, blocking collectives, on_device(): pieces = lax.all_to_all(pieces, 'rep', split_axis=0, concat_axis=0)  46.8 us
    ppermute x7, starting transfers between devices, shifted(): return lax.ppermute(x, axis, pairs)  36.6 us
    reduce_scatter x1, waiting for transfers between devices, on_device(): lax.psum_scatter(contribution.astype(jnp.bfloat16), 'section', scatter_di...  33.1 us
    all_to_all x1, waiting for transfers between devices, on_device(): lax.all_to_all(outgoing, 'rep', split_axis=1, concat_axis=1, tiled=True)  28.9 us
    dot_general x4, matrix products, update(): jnp.einsum('nscd,sde->nsce', lowered, section_weight, preferred_element_t...  17.4 us
    select_n x14, local copies, waits for them, and re-layouts, tick(): outbuf = jnp.where(storing, stored, outbuf)  17.3 us
    split x1, local copies, waits for them, and re-layouts, on_device(): pieces = jnp.stack(jnp.split(value, size, axis=1), axis=0)  14.2 us
  transfers between devices with their start and end apart: 9, of which 9 were waited for; matrix products, arithmetic and copies ran while one was open for 4% of the time, Pallas kernels for 0%

profile of v1, /device:TPU:0, one launch (start us, length us, event | category | flops | bytes accessed | tf_op | source)
XLA Modules:
  0.0 289.3 jit_solution(1530068219935787646)
XLA Ops:
  6.5 0.8 select_reduce_fusion.2
  8.0 2.1 convolution_convert_fusion
  10.1 3.2 %copy.188 = bf16[4,288,1024]{2,0,1:T(4,128)(2,1)} copy(bf16[4,288,1024]{2,1,0:T(8,128)(2,1)S(1)} %convolution_convert_fusion) | data formatting | bytes 4718592 | tf_op jit(solution)/shard_map/convert_element_type | solution.py:75
  13.4 5.3 %all-to-all-start = ((bf16[4,8,36,1024]{3,0,2,1:T(4,128)(2,1)}), bf16[4,8,36,1024]{3,0,2,1:T(4,128)(2,1)S(1)}, u32[]{:S(2)}, u32[]{:S(2)}) async-start(bf16[4,8,36,1024]{3,0,2,1:T(4,128)(2,1)} %bitcast.55), calls=%async_computation | async-start | bytes 4718592 | tf_op jit(solution)/shard_map/all_to_all | solution.py:77
  19.2 28.9 %all-to-all-done = bf16[4,8,36,1024]{3,0,2,1:T(4,128)(2,1)S(1)} async-done(((bf16[4,8,36,1024]{3,0,2,1:T(4,128)(2,1)}), bf16[4,8,36,1024]{3,0,2,1:T(4,128)(2,1)S(1)}, u32[]{:S(2)}, u32[]{:S(2)}) %all-to-all-start) | async-done | bytes 2359328 | tf_op jit(solution)/shard_map/all_to_all | solution.py:77
  48.1 2.7 copy.189
  50.9 1.7 broadcast_in_dim.47.clone
  52.6 129.9 %while.17 = (s32[]{:T(128)}, bf16[8,3,12,1024]{3,0,2,1:T(8,128)(2,1)S(1)}, bf16[4,8,3,12,1024]{4,1,3,2,0:T(8,128)(2,1)}, s32[]{:T(128)}, pred[]{:T(512)}, /*inde...) while((s32[]{:T(128)}, ...), condition=%wide.region_9.10_spmd.clone, body=%wide.region_5.9_spmd.clone.sunk | while | flops 608999680 | bytes 19899208 | solution.py:96
  52.6 1.3 constant_dynamic-slice_fusion.3
  54.0 0.6 bitcast_select_fusion.2
  54.6 4.7 %conditional.3 = (bf16[8,3,12,1024]{3,2,0,1:T(8,128)(2,1)S(1)}) conditional(s32[]{:T(128)} %convert_element_type.86, bf16[8,3,12,1024]{3,2,0,1:T(8,128)(2,1)S(1)} %bitcast_select_fusion.2, (bf16[8,3,12,1024]{3,2,0,1:T(8,128)(2,1)S(1)}, f32[3]{0:T(128)S(1)}, f32[1,3,1024]{2,1,0:T(4,128)S(1)}, bf16[3,1024,1024]{2,1,0:T(8,128)(2,1)}, ...), branch_computations={%region_6.6_spmd, %region_7.8_spmd} | conditional | flops 608403712 | bytes 9269780 | solution.py:87
  55.0 4.3 %fusion.7 = bf16[8,3,12,1024]{3,2,0,1:T(8,128)(2,1)S(1)} fusion(bf16[8,3,12,1024]{3,2,0,1:T(8,128)(2,1)S(1)} %copy.253, bf16[3,1024,1024]{2,1,0:T(8,128)(2,1)} %get-tuple-element.218, f32[3,1024]{1,0:T(4,128)S(1)} %get-tuple-element.219, f32[3,1024]{1,0:T(4,128)S(1)} %bitcast.57, f32[8,3,12]{2,0,1:T(8,128)S(1)} %add_rsqrt_fusion), kind=kOutput, calls=%fused_computation.9 | convolution fusion | flops 607518720 | bytes 7496832 | tf_op jit(solution)/shard_map/while/body/eval_jaxpr/cond/branch_1_fun/nscd,sde->nsce/dot_general | solution.py:58
  59.7 1.3 collective-permute-start
  61.0 0.4 copy_select_fusion.2
  61.4 1.2 copy_dynamic-update-slice_fusion.2
  62.6 8.6 %collective-permute-done = bf16[8,3,12,1024]{3,0,2,1:T(8,128)(2,1)S(1)} collective-permute-done((bf16[8,3,12,1024]{3,0,2,1:T(8,128)(2,1)S(1)}, bf16[8,3,12,1024]{3,0,2,1:T(8,128)(2,1)S(1)}, u32[]{:S(2)}, u32[]{:S(2)}) %collective-permute-start) | collective-permute-done | bytes 589856 | tf_op jit(solution)/shard_map/while/body/eval_jaxpr/ppermute | solution.py:12
  71.2 1.3 constant_dynamic-slice_fusion.3
  72.5 0.6 bitcast_select_fusion.2
  73.2 4.8 %conditional.3 = (bf16[8,3,12,1024]{3,2,0,1:T(8,128)(2,1)S(1)}) conditional(s32[]{:T(128)} %convert_element_type.86, bf16[8,3,12,1024]{3,2,0,1:T(8,128)(2,1)S(1)} %bitcast_select_fusion.2, (bf16[8,3,12,1024]{3,2,0,1:T(8,128)(2,1)S(1)}, f32[3]{0:T(128)S(1)}, f32[1,3,1024]{2,1,0:T(4,128)S(1)}, bf16[3,1024,1024]{2,1,0:T(8,128)(2,1)}, ...), branch_computations={%region_6.6_spmd, %region_7.8_spmd} | conditional | flops 608403712 | bytes 9269780 | solution.py:87
  73.6 4.4 %fusion.7 = bf16[8,3,12,1024]{3,2,0,1:T(8,128)(2,1)S(1)} fusion(bf16[8,3,12,1024]{3,2,0,1:T(8,128)(2,1)S(1)} %copy.253, bf16[3,1024,1024]{2,1,0:T(8,128)(2,1)} %get-tuple-element.218, f32[3,1024]{1,0:T(4,128)S(1)} %get-tuple-element.219, f32[3,1024]{1,0:T(4,128)S(1)} %bitcast.57, f32[8,3,12]{2,0,1:T(8,128)S(1)} %add_rsqrt_fusion), kind=kOutput, calls=%fused_computation.9 | convolution fusion | flops 607518720 | bytes 7496832 | tf_op jit(solution)/shard_map/while/body/eval_jaxpr/cond/branch_1_fun/nscd,sde->nsce/dot_general | solution.py:58
  78.3 4.4 %collective-permute-start = (bf16[8,3,12,1024]{3,0,2,1:T(8,128)(2,1)S(1)}, bf16[8,3,12,1024]{3,0,2,1:T(8,128)(2,1)S(1)}, u32[]{:S(2)}, u32[]{:S(2)}) collective-permute-start(bf16[8,3,12,1024]{3,0,2,1:T(8,128)(2,1)S(1)} %copy.232), channel_id=1, source_target_pairs={{0,8},{8,16},{16,24},{1,9},{9,17},{17,25},{2,10},{10,18},{18,26},{... | collective-permute-start | bytes 1769480 | tf_op jit(solution)/shard_map/while/body/eval_jaxpr/ppermute | solution.py:12
  83.1 1.2 copy_dynamic-update-slice_fusion.2
  84.2 7.7 %collective-permute-done = bf16[8,3,12,1024]{3,0,2,1:T(8,128)(2,1)S(1)} collective-permute-done((bf16[8,3,12,1024]{3,0,2,1:T(8,128)(2,1)S(1)}, bf16[8,3,12,1024]{3,0,2,1:T(8,128)(2,1)S(1)}, u32[]{:S(2)}, u32[]{:S(2)}) %collective-permute-start) | collective-permute-done | bytes 589856 | tf_op jit(solution)/shard_map/while/body/eval_jaxpr/ppermute | solution.py:12
  92.0 1.3 constant_dynamic-slice_fusion.3
  93.3 0.6 bitcast_select_fusion.2
  94.0 4.8 %conditional.3 = (bf16[8,3,12,1024]{3,2,0,1:T(8,128)(2,1)S(1)}) conditional(s32[]{:T(128)} %convert_element_type.86, bf16[8,3,12,1024]{3,2,0,1:T(8,128)(2,1)S(1)} %bitcast_select_fusion.2, (bf16[8,3,12,1024]{3,2,0,1:T(8,128)(2,1)S(1)}, f32[3]{0:T(128)S(1)}, f32[1,3,1024]{2,1,0:T(4,128)S(1)}, bf16[3,1024,1024]{2,1,0:T(8,128)(2,1)}, ...), branch_computations={%region_6.6_spmd, %region_7.8_spmd} | conditional | flops 608403712 | bytes 9269780 | solution.py:87
  94.4 4.4 %fusion.7 = bf16[8,3,12,1024]{3,2,0,1:T(8,128)(2,1)S(1)} fusion(bf16[8,3,12,1024]{3,2,0,1:T(8,128)(2,1)S(1)} %copy.253, bf16[3,1024,1024]{2,1,0:T(8,128)(2,1)} %get-tuple-element.218, f32[3,1024]{1,0:T(4,128)S(1)} %get-tuple-element.219, f32[3,1024]{1,0:T(4,128)S(1)} %bitcast.57, f32[8,3,12]{2,0,1:T(8,128)S(1)} %add_rsqrt_fusion), kind=kOutput, calls=%fused_computation.9 | convolution fusion | flops 607518720 | bytes 7496832 | tf_op jit(solution)/shard_map/while/body/eval_jaxpr/cond/branch_1_fun/nscd,sde->nsce/dot_general | solution.py:58
  99.1 4.4 %collective-permute-start = (bf16[8,3,12,1024]{3,0,2,1:T(8,128)(2,1)S(1)}, bf16[8,3,12,1024]{3,0,2,1:T(8,128)(2,1)S(1)}, u32[]{:S(2)}, u32[]{:S(2)}) collective-permute-start(bf16[8,3,12,1024]{3,0,2,1:T(8,128)(2,1)S(1)} %copy.232), channel_id=1, source_target_pairs={{0,8},{8,16},{16,24},{1,9},{9,17},{17,25},{2,10},{10,18},{18,26},{... | collective-permute-start | bytes 1769480 | tf_op jit(solution)/shard_map/while/body/eval_jaxpr/ppermute | solution.py:12
  103.9 1.2 copy_dynamic-update-slice_fusion.2
  105.0 6.9 %collective-permute-done = bf16[8,3,12,1024]{3,0,2,1:T(8,128)(2,1)S(1)} collective-permute-done((bf16[8,3,12,1024]{3,0,2,1:T(8,128)(2,1)S(1)}, bf16[8,3,12,1024]{3,0,2,1:T(8,128)(2,1)S(1)}, u32[]{:S(2)}, u32[]{:S(2)}) %collective-permute-start) | collective-permute-done | bytes 589856 | tf_op jit(solution)/shard_map/while/body/eval_jaxpr/ppermute | solution.py:12
  111.9 1.3 constant_dynamic-slice_fusion.3
  113.3 0.6 bitcast_select_fusion.2
  113.9 4.8 %conditional.3 = (bf16[8,3,12,1024]{3,2,0,1:T(8,128)(2,1)S(1)}) conditional(s32[]{:T(128)} %convert_element_type.86, bf16[8,3,12,1024]{3,2,0,1:T(8,128)(2,1)S(1)} %bitcast_select_fusion.2, (bf16[8,3,12,1024]{3,2,0,1:T(8,128)(2,1)S(1)}, f32[3]{0:T(128)S(1)}, f32[1,3,1024]{2,1,0:T(4,128)S(1)}, bf16[3,1024,1024]{2,1,0:T(8,128)(2,1)}, ...), branch_computations={%region_6.6_spmd, %region_7.8_spmd} | conditional | flops 608403712 | bytes 9269780 | solution.py:87
  114.3 4.4 %fusion.7 = bf16[8,3,12,1024]{3,2,0,1:T(8,128)(2,1)S(1)} fusion(bf16[8,3,12,1024]{3,2,0,1:T(8,128)(2,1)S(1)} %copy.253, bf16[3,1024,1024]{2,1,0:T(8,128)(2,1)} %get-tuple-element.218, f32[3,1024]{1,0:T(4,128)S(1)} %get-tuple-element.219, f32[3,1024]{1,0:T(4,128)S(1)} %bitcast.57, f32[8,3,12]{2,0,1:T(8,128)S(1)} %add_rsqrt_fusion), kind=kOutput, calls=%fused_computation.9 | convolution fusion | flops 607518720 | bytes 7496832 | tf_op jit(solution)/shard_map/while/body/eval_jaxpr/cond/branch_1_fun/nscd,sde->nsce/dot_general | solution.py:58
  119.0 4.4 %collective-permute-start = (bf16[8,3,12,1024]{3,0,2,1:T(8,128)(2,1)S(1)}, bf16[8,3,12,1024]{3,0,2,1:T(8,128)(2,1)S(1)}, u32[]{:S(2)}, u32[]{:S(2)}) collective-permute-start(bf16[8,3,12,1024]{3,0,2,1:T(8,128)(2,1)S(1)} %copy.232), channel_id=1, source_target_pairs={{0,8},{8,16},{16,24},{1,9},{9,17},{17,25},{2,10},{10,18},{18,26},{... | collective-permute-start | bytes 1769480 | tf_op jit(solution)/shard_map/while/body/eval_jaxpr/ppermute | solution.py:12
  123.8 1.2 copy_dynamic-update-slice_fusion.2
  125.0 6.0 %collective-permute-done = bf16[8,3,12,1024]{3,0,2,1:T(8,128)(2,1)S(1)} collective-permute-done((bf16[8,3,12,1024]{3,0,2,1:T(8,128)(2,1)S(1)}, bf16[8,3,12,1024]{3,0,2,1:T(8,128)(2,1)S(1)}, u32[]{:S(2)}, u32[]{:S(2)}) %collective-permute-start) | collective-permute-done | bytes 589856 | tf_op jit(solution)/shard_map/while/body/eval_jaxpr/ppermute | solution.py:12
  131.0 1.3 constant_dynamic-slice_fusion.3
  132.4 0.6 bitcast_select_fusion.2
  133.4 9.2 %collective-permute-start = (bf16[8,3,12,1024]{3,0,2,1:T(8,128)(2,1)S(1)}, bf16[8,3,12,1024]{3,0,2,1:T(8,128)(2,1)S(1)}, u32[]{:S(2)}, u32[]{:S(2)}) collective-permute-start(bf16[8,3,12,1024]{3,0,2,1:T(8,128)(2,1)S(1)} %copy.232), channel_id=1, source_target_pairs={{0,8},{8,16},{16,24},{1,9},{9,17},{17,25},{2,10},{10,18},{18,26},{... | collective-permute-start | bytes 1769480 | tf_op jit(solution)/shard_map/while/body/eval_jaxpr/ppermute | solution.py:12
  142.9 1.2 copy_dynamic-update-slice_fusion.2
  144.0 6.1 %collective-permute-done = bf16[8,3,12,1024]{3,0,2,1:T(8,128)(2,1)S(1)} collective-permute-done((bf16[8,3,12,1024]{3,0,2,1:T(8,128)(2,1)S(1)}, bf16[8,3,12,1024]{3,0,2,1:T(8,128)(2,1)S(1)}, u32[]{:S(2)}, u32[]{:S(2)}) %collective-permute-start) | collective-permute-done | bytes 589856 | tf_op jit(solution)/shard_map/while/body/eval_jaxpr/ppermute | solution.py:12
  150.2 1.3 constant_dynamic-slice_fusion.3
  151.6 0.6 bitcast_select_fusion.2
  152.6 4.4 %collective-permute-start = (bf16[8,3,12,1024]{3,0,2,1:T(8,128)(2,1)S(1)}, bf16[8,3,12,1024]{3,0,2,1:T(8,128)(2,1)S(1)}, u32[]{:S(2)}, u32[]{:S(2)}) collective-permute-start(bf16[8,3,12,1024]{3,0,2,1:T(8,128)(2,1)S(1)} %copy.232), channel_id=1, source_target_pairs={{0,8},{8,16},{16,24},{1,9},{9,17},{17,25},{2,10},{10,18},{18,26},{... | collective-permute-start | bytes 1769480 | tf_op jit(solution)/shard_map/while/body/eval_jaxpr/ppermute | solution.py:12
  157.4 1.2 copy_dynamic-update-slice_fusion.2
  158.5 5.8 %collective-permute-done = bf16[8,3,12,1024]{3,0,2,1:T(8,128)(2,1)S(1)} collective-permute-done((bf16[8,3,12,1024]{3,0,2,1:T(8,128)(2,1)S(1)}, bf16[8,3,12,1024]{3,0,2,1:T(8,128)(2,1)S(1)}, u32[]{:S(2)}, u32[]{:S(2)}) %collective-permute-start) | collective-permute-done | bytes 589856 | tf_op jit(solution)/shard_map/while/body/eval_jaxpr/ppermute | solution.py:12
  164.4 1.3 constant_dynamic-slice_fusion.3
  165.7 0.6 bitcast_select_fusion.2
  166.7 8.4 %collective-permute-start = (bf16[8,3,12,1024]{3,0,2,1:T(8,128)(2,1)S(1)}, bf16[8,3,12,1024]{3,0,2,1:T(8,128)(2,1)S(1)}, u32[]{:S(2)}, u32[]{:S(2)}) collective-permute-start(bf16[8,3,12,1024]{3,0,2,1:T(8,128)(2,1)S(1)} %copy.232), channel_id=1, source_target_pairs={{0,8},{8,16},{16,24},{1,9},{9,17},{17,25},{2,10},{10,18},{18,26},{... | collective-permute-start | bytes 1769480 | tf_op jit(solution)/shard_map/while/body/eval_jaxpr/ppermute | solution.py:12
  175.5 1.2 copy_dynamic-update-slice_fusion.2
  176.7 5.8 %collective-permute-done = bf16[8,3,12,1024]{3,0,2,1:T(8,128)(2,1)S(1)} collective-permute-done((bf16[8,3,12,1024]{3,0,2,1:T(8,128)(2,1)S(1)}, bf16[8,3,12,1024]{3,0,2,1:T(8,128)(2,1)S(1)}, u32[]{:S(2)}, u32[]{:S(2)}) %collective-permute-start) | collective-permute-done | bytes 589856 | tf_op jit(solution)/shard_map/while/body/eval_jaxpr/ppermute | solution.py:12
  182.5 14.2 %fusion.35 = (bf16[4,1,36,1024]{3,1,2,0:T(2,128)(2,1)S(1)}, bf16[4,1,36,1024]{3,1,2,0:T(2,128)(2,1)S(1)}, bf16[4,1,36,1024]{3,1,2,0:T(2,128)(2,1)S(1)}, bf16[4,1...) fusion(bf16[4,8,36,1024]{3,1,2,0:T(8,128)(2,1)} %bitcast.8), kind=kLoop, calls=%fused_computation.57 | loop fusion | bytes 4718592 | tf_op jit(solution)/shard_map/split | solution.py:99
  196.7 0.4 bitcast_dynamic-update-slice_fusion.7
  197.1 0.4 bitcast_dynamic-update-slice_fusion.6
  197.5 0.4 bitcast_dynamic-update-slice_fusion.5
  197.9 0.4 bitcast_dynamic-update-slice_fusion.4
  198.3 0.4 bitcast_dynamic-update-slice_fusion.3
  198.7 0.4 bitcast_dynamic-update-slice_fusion.2
  199.1 0.4 bitcast_dynamic-update-slice_fusion.1
  199.5 0.4 bitcast_dynamic-update-slice_fusion
  199.9 46.8 %all_to_all.10 = bf16[8,4,1,36,1024]{4,1,3,2,0:T(4,128)(2,1)S(1)} all-to-all(bf16[8,4,1,36,1024]{4,1,3,2,0:T(4,128)(2,1)S(1)} %bitcast_dynamic-update-slice_fusion), channel_id=1, replica_groups=mesh['section'=4,'rep'=8] {'rep'}, dimensions={0} | all-to-all | bytes 4718592 | tf_op jit(solution)/shard_map/all_to_all | solution.py:100
  246.8 2.6 select_convert_fusion
  249.4 33.1 %reduce-scatter.2.cloned.1.call-done = bf16[4,128,256]{2,1,0:T(8,128)(2,1)} async-done(((bf16[4,128,1024]{2,1,0:T(8,128)(2,1)}), bf16[4,128,256]{2,1,0:T(8,128)(2,1)}) %reduce-scatter.2.cloned.1.call-update) | async-done | bytes 262160 | tf_op jit(solution)/shard_map/reduce_scatter | solution.py:109
  (52 shorter events, 7.7 us)
Async XLA Ops:
  13.3 5.6 %copy-start = (f32[1,3,1024]{2,0,1:T(1,128)S(1)}, f32[1,3,1024]{2,0,1:T(1,128)}, u32[]{:S(2)}) copy-start(f32[1,3,1024]{2,0,1:T(1,128)} %param.14) | copy-start | bytes 36868
  13.3 5.6 %copy-start.1 = (s32[16]{0:T(128)S(1)}, s32[16]{0:T(128)}, u32[]{:S(2)}) copy-start(s32[16]{0:T(128)} %param.13) | copy-start | bytes 196
  13.3 5.6 %copy-start.2 = (s32[16]{0:T(128)S(1)}, s32[16]{0:T(128)}, u32[]{:S(2)}) copy-start(s32[16]{0:T(128)} %param.12) | copy-start | bytes 196
  13.4 34.8 %all-to-all-start = ((bf16[4,8,36,1024]{3,0,2,1:T(4,128)(2,1)}), bf16[4,8,36,1024]{3,0,2,1:T(4,128)(2,1)S(1)}, u32[]{:S(2)}, u32[]{:S(2)}) async-start(bf16[4,8,36,1024]{3,0,2,1:T(4,128)(2,1)} %bitcast.55), calls=%async_computation | async-start | bytes 4718592 | tf_op jit(solution)/shard_map/all_to_all | solution.py:77
  18.7 263.8 %reduce-scatter.2.cloned.1.call-start = ((), (), s32[]{:S(2)}) async-start(), calls=%async_computation.3 | async-start | bytes 1310720 | tf_op jit(solution)/shard_map/reduce_scatter | solution.py:109
  59.7 11.4 %collective-permute-start = (bf16[8,3,12,1024]{3,0,2,1:T(8,128)(2,1)S(1)}, bf16[8,3,12,1024]{3,0,2,1:T(8,128)(2,1)S(1)}, u32[]{:S(2)}, u32[]{:S(2)}) collective-permute-start(bf16[8,3,12,1024]{3,0,2,1:T(8,128)(2,1)S(1)} %copy.232), channel_id=1, source_target_pairs={{0,8},{8,16},{16,24},{1,9},{9,17},{17,25},{2,10},{10,18},{18,26},{... | collective-permute-start | bytes 1769480 | tf_op jit(solution)/shard_map/while/body/eval_jaxpr/ppermute | solution.py:12
  78.3 13.6 %collective-permute-start = (bf16[8,3,12,1024]{3,0,2,1:T(8,128)(2,1)S(1)}, bf16[8,3,12,1024]{3,0,2,1:T(8,128)(2,1)S(1)}, u32[]{:S(2)}, u32[]{:S(2)}) collective-permute-start(bf16[8,3,12,1024]{3,0,2,1:T(8,128)(2,1)S(1)} %copy.232), channel_id=1, source_target_pairs={{0,8},{8,16},{16,24},{1,9},{9,17},{17,25},{2,10},{10,18},{18,26},{... | collective-permute-start | bytes 1769480 | tf_op jit(solution)/shard_map/while/body/eval_jaxpr/ppermute | solution.py:12
  99.1 12.8 %collective-permute-start = (bf16[8,3,12,1024]{3,0,2,1:T(8,128)(2,1)S(1)}, bf16[8,3,12,1024]{3,0,2,1:T(8,128)(2,1)S(1)}, u32[]{:S(2)}, u32[]{:S(2)}) collective-permute-start(bf16[8,3,12,1024]{3,0,2,1:T(8,128)(2,1)S(1)} %copy.232), channel_id=1, source_target_pairs={{0,8},{8,16},{16,24},{1,9},{9,17},{17,25},{2,10},{10,18},{18,26},{... | collective-permute-start | bytes 1769480 | tf_op jit(solution)/shard_map/while/body/eval_jaxpr/ppermute | solution.py:12
  119.0 11.9 %collective-permute-start = (bf16[8,3,12,1024]{3,0,2,1:T(8,128)(2,1)S(1)}, bf16[8,3,12,1024]{3,0,2,1:T(8,128)(2,1)S(1)}, u32[]{:S(2)}, u32[]{:S(2)}) collective-permute-start(bf16[8,3,12,1024]{3,0,2,1:T(8,128)(2,1)S(1)} %copy.232), channel_id=1, source_target_pairs={{0,8},{8,16},{16,24},{1,9},{9,17},{17,25},{2,10},{10,18},{18,26},{... | collective-permute-start | bytes 1769480 | tf_op jit(solution)/shard_map/while/body/eval_jaxpr/ppermute | solution.py:12
  133.4 16.8 %collective-permute-start = (bf16[8,3,12,1024]{3,0,2,1:T(8,128)(2,1)S(1)}, bf16[8,3,12,1024]{3,0,2,1:T(8,128)(2,1)S(1)}, u32[]{:S(2)}, u32[]{:S(2)}) collective-permute-start(bf16[8,3,12,1024]{3,0,2,1:T(8,128)(2,1)S(1)} %copy.232), channel_id=1, source_target_pairs={{0,8},{8,16},{16,24},{1,9},{9,17},{17,25},{2,10},{10,18},{18,26},{... | collective-permute-start | bytes 1769480 | tf_op jit(solution)/shard_map/while/body/eval_jaxpr/ppermute | solution.py:12
  152.6 11.8 %collective-permute-start = (bf16[8,3,12,1024]{3,0,2,1:T(8,128)(2,1)S(1)}, bf16[8,3,12,1024]{3,0,2,1:T(8,128)(2,1)S(1)}, u32[]{:S(2)}, u32[]{:S(2)}) collective-permute-start(bf16[8,3,12,1024]{3,0,2,1:T(8,128)(2,1)S(1)} %copy.232), channel_id=1, source_target_pairs={{0,8},{8,16},{16,24},{1,9},{9,17},{17,25},{2,10},{10,18},{18,26},{... | collective-permute-start | bytes 1769480 | tf_op jit(solution)/shard_map/while/body/eval_jaxpr/ppermute | solution.py:12
  166.7 15.8 %collective-permute-start = (bf16[8,3,12,1024]{3,0,2,1:T(8,128)(2,1)S(1)}, bf16[8,3,12,1024]{3,0,2,1:T(8,128)(2,1)S(1)}, u32[]{:S(2)}, u32[]{:S(2)}) collective-permute-start(bf16[8,3,12,1024]{3,0,2,1:T(8,128)(2,1)S(1)} %copy.232), channel_id=1, source_target_pairs={{0,8},{8,16},{16,24},{1,9},{9,17},{17,25},{2,10},{10,18},{18,26},{... | collective-permute-start | bytes 1769480 | tf_op jit(solution)/shard_map/while/body/eval_jaxpr/ppermute | solution.py:12
Sparse Core Ops, SparseCore 0:
  249.5 32.9 reduce-scatter.1
